TPU v7x, 32 devices: a whole 2x2x4 slice. The times are simulated.
32 devices in a mesh: front: 4 (over x, core), grid: 8 (over z, y).
Axes of the slice: x: 2, y: 2, z: 4, core: 2. Of those that a mesh axis runs over, the one named last changes fastest.
Arguments:
- index_map: int32 [4, 8192], P('front'), may hold values from 0 to 16383, as said below
- lengths: int32 [4], P('front'), may hold values from 1 to 8192, 24576 in all
- update_front: float32 [4, 8192, 8192], P('front', 'grid'), may hold values from -0.0625 to 0.0625
- front_matrix: float32 [16384, 16384], P(('front', 'grid')), may hold values from -0.046875 to 0.046875
- random: float32 [16384, 256], P(('front', 'grid')), may hold values from -6 to 6
Outputs:
- parent_sample: float32 [16384, 256], P(('front', 'grid'))
Inputs may be any that keep to these rules, and one draw needn't show every extreme that they name: `index_map`: within one child the 8192 entries are distinct parent rows. `lengths`: rows of a child at or past its length are not live; the largest length equals 8192.
All inputs are finite; a program needn't handle non-finite values. No bound on the sum of `lengths` on one device may be relied on, other than what follows from the above.
Results may differ from a plain program's by a relative error of at most 0.0003.
Values sent between devices are 32-bit elements; how exact they have to be, the bound alone decides.
A program may use at most 192 MiB of HBM per device.

v0:
```python
import jax
import jax.numpy as jnp
from jax import lax
from jax.sharding import PartitionSpec as P


def shards(index_map, lengths, update_front, front_matrix, random):
    gathered_random = lax.all_gather(random, ("front", "grid"), axis=0, tiled=True)
    parent_part = jnp.dot(
        front_matrix,
        gathered_random,
        preferred_element_type=jnp.float32,
        precision=lax.Precision.HIGHEST,
    )
    index_rows = index_map[0]
    child_random = jnp.take(gathered_random, index_rows, axis=0)
    child_sample = jnp.dot(
        update_front[0],
        child_random,
        preferred_element_type=jnp.float32,
        precision=lax.Precision.HIGHEST,
    )
    local_rows = child_sample.shape[0]
    first_row = lax.axis_index("grid") * local_rows
    row_numbers = first_row + jnp.arange(local_rows, dtype=jnp.int32)
    live_rows = row_numbers < lengths[0]
    child_sample = jnp.where(live_rows[:, None], child_sample, jnp.float32(0.0))
    own_rows = parent_part.shape[0]
    group_sample = lax.all_gather(child_sample, "grid", axis=0, tiled=True)
    group_count = lax.axis_size("front")
    grid_count = lax.axis_size("grid")
    grid_place = lax.axis_index("grid")
    block_ids = jnp.arange(group_count, dtype=jnp.int32)[:, None] * grid_count + grid_place
    targets = (block_ids * own_rows + jnp.arange(own_rows, dtype=jnp.int32)[None, :]).reshape(-1)
    one_hot = (targets[:, None] == index_rows[None, :]).astype(jnp.float32)
    terms = jnp.dot(
        one_hot, group_sample, preferred_element_type=jnp.float32, precision=lax.Precision.HIGHEST
    )
    terms = terms.reshape(group_count, own_rows, terms.shape[1])
    added = lax.psum_scatter(terms, "front", scatter_dimension=0, tiled=True)[0]
    return parent_part + added


def solution(mesh):
    placed = (
        P("front", None),
        P("front"),
        P("front", "grid", None),
        P(("front", "grid"), None),
        P(("front", "grid"), None),
    )
    return jax.shard_map(
        shards, mesh=mesh, in_specs=placed, out_specs=P(("front", "grid"), None), check_vma=False
    )
```

profile of v0, /device:TPU:0, one launch (start us, length us, event | category | flops | bytes accessed | tf_op | source)
XLA Modules:
  0.0 452.4 jit_solution(5761068284359675660)
XLA Ops:
  6.5 0.0 all-gather.3.cloned.1.call-start
  6.5 0.7 all-gather.3.cloned.1.call-update
  7.3 0.0 all-gather.5.cloned.1.call-start
  8.0 0.8 compare_and_fusion
  8.7 0.8 compare_select_fusion
  9.6 118.0 %all-gather.3.cloned.1.call-done = f32[16384,256]{1,0:T(8,128)} async-done(((f32[512,256]{1,0:T(8,128)}), f32[16384,256]{1,0:T(8,128)}) %all-gather.3.cloned.1.call-update) | async-done | bytes 16777232 | tf_op jit(solution)/shard_map/all_gather | solution.py:8
  127.5 37.1 %gather_fusion = f32[8192,256]{1,0:T(8,128)} fusion(f32[16384,256]{1,0:T(8,128)} %all-gather.3.cloned.1.call-done, s32[8192]{0:T(1024)S(1)} %broadcast_clamp_fusion), kind=kCustom, calls=%fused_computation | custom fusion | bytes 16809984 | tf_op jit(solution)/shard_map/jit(_take)/gather | solution.py:16
  164.7 0.0 copy-start
  164.7 59.7 %fusion.14 = f32[1024,256]{0,1:T(8,128)} fusion(f32[1,1024,8192]{2,1,0:T(8,128)} %param.7, f32[8192,256]{1,0:T(8,128)} %gather_fusion, pred[8192]{0:T(1024)(128)(4,1)S(1)} %compare_and_fusion, pred[1024]{0:T(1024)(128)(4,1)S(1)} %add_compare_fusion), kind=kOutput, calls=%fused_computation.11 | convolution fusion | flops 25772163072 | bytes 43000832 | tf_op jit(solution)/shard_map/dot_general | solution.py:17
  224.3 0.0 all-gather.5.cloned.1.call-update
  224.3 0.2 reduce-scatter.2.cloned.1.call-start
  224.6 0.1 add_bitcast_fusion
  224.7 122.5 %all-gather.5.cloned.1.call-done = f32[8192,256]{0,1:T(8,128)} async-done(((f32[1024,256]{0,1:T(8,128)}), f32[8192,256]{0,1:T(8,128)}) %all-gather.5.cloned.1.call-update) | async-done | bytes 8388624 | tf_op jit(solution)/shard_map/all_gather | solution.py:29
  347.2 0.0 copy-done
  347.2 36.9 %fusion = f32[2048,256]{1,0:T(8,128)} fusion(f32[8192,256]{0,1:T(8,128)} %all-gather.5.cloned.1.call-done, s32[8192]{0:T(1024)S(1)} %bitcast.26, s32[2048]{0:T(1024)S(1)} %bitcast.28), kind=kOutput, calls=%fused_computation.1 | convolution fusion | flops 51556384768 | bytes 10526720 | tf_op jit(solution)/shard_map/dot_general | solution.py:36
  384.1 0.0 reduce-scatter.2.cloned.1.call-update
  384.1 29.5 %reduce-scatter.2.cloned.1.call-done = f32[1,512,256]{2,1,0:T(8,128)} async-done(((f32[4,512,256]{2,1,0:T(8,128)}), f32[1,512,256]{2,1,0:T(8,128)}) %reduce-scatter.2.cloned.1.call-update) | async-done | bytes 524304 | tf_op jit(solution)/shard_map/reduce_scatter | solution.py:40
  413.6 32.3 %convolution_add_fusion = f32[512,256]{1,0:T(8,128)} fusion(f32[512,16384]{1,0:T(8,128)} %param.8, f32[16384,256]{1,0:T(8,128)} %all-gather.3.cloned.1.call-done, f32[1,512,256]{2,1,0:T(8,128)} %reduce-scatter.2.cloned.1.call-done), kind=kOutput, calls=%fused_computation.12 | convolution fusion | flops 25769934848 | bytes 51380224 | tf_op jit(solution)/shard_map/dot_general | solution.py:9
  (4 shorter events, 0.0 us)
Async XLA Ops:
  6.5 121.0 %all-gather.3.cloned.1.call-start = ((), (), s32[]{:S(2)}) async-start(), calls=%async_computation.1 | async-start | bytes 17301504 | tf_op jit(solution)/shard_map/all_gather | solution.py:8
  7.3 339.9 %all-gather.5.cloned.1.call-start = ((), (), s32[]{:S(2)}) async-start(), calls=%async_computation.2 | async-start | bytes 9437184 | tf_op jit(solution)/shard_map/all_gather | solution.py:29
  164.7 182.5 %copy-start = (s32[1,8192]{1,0:T(1,128)S(1)}, s32[1,8192]{1,0:T(1,128)}, u32[]{:S(2)}) copy-start(s32[1,8192]{1,0:T(1,128)} %param.5) | copy-start | bytes 98308
  224.3 189.2 %reduce-scatter.2.cloned.1.call-start = ((), (), s32[]{:S(2)}) async-start(), calls=%async_computation.3 | async-start | bytes 2621440 | tf_op jit(solution)/shard_map/reduce_scatter | solution.py:40
Sparse Core Ops, SparseCore 0:
  10.4 117.0 all-gather.2
  224.5 122.6 all-gather.4
  384.2 29.3 reduce-scatter.1
where the time goes:
time: 453 us; the launch traced here: 452 us
  waiting for transfers between devices  271 us (60%)
  matrix products  129 us (28%)
  local copies, waits for them, and re-layouts  37.2 us (8%)
  between operations  13.8 us (3%)
    all_gather x1, waiting for transfers between devices, shards(): group_sample = lax.all_gather(child_sample, 'grid', axis=0, tiled=True)  123 us
    all_gather x1, waiting for transfers between devices, shards(): lax.all_gather(random, ('front', 'grid'), axis=0, tiled=True)  118 us
    dot_general x1, matrix products, shards(): jnp.dot(update_front[0], child_random, preferred_element_type=jnp.float32...  59.7 us
    gather x1, local copies, waits for them, and re-layouts, shards(): child_random = jnp.take(gathered_random, index_rows, axis=0)  37.1 us
    dot_general x1, matrix products, shards(): jnp.dot(one_hot, group_sample, preferred_element_type=jnp.float32, precis...  36.9 us
    dot_general x1, matrix products, shards(): jnp.dot(front_matrix, gathered_random, preferred_element_type=jnp.float32...  32.3 us
    reduce_scatter x1, waiting for transfers between devices, shards(): added = lax.psum_scatter(terms, 'front', scatter_dimension=0, tiled=True)[0]  29.5 us
  transfers between devices with their start and end apart: 3, of which 3 were waited for; matrix products, arithmetic and copies ran while one was open for 0% of the time, Pallas kernels for 0%

commit v1 on v0

--- a/solution.py
+++ b/solution.py
@@ -26,7 +26,10 @@
     live_rows = row_numbers < lengths[0]
     child_sample = jnp.where(live_rows[:, None], child_sample, jnp.float32(0.0))
     own_rows = parent_part.shape[0]
-    group_sample = lax.all_gather(child_sample, "grid", axis=0, tiled=True)
+    size = lax.axis_size("grid")
+    pieces = jnp.stack([child_sample for _ in range(size)])
+    pieces = lax.all_to_all(pieces, "grid", split_axis=0, concat_axis=0)
+    group_sample = jnp.concatenate(pieces, axis=0)
     group_count = lax.axis_size("front")
     grid_count = lax.axis_size("grid")
     grid_place = lax.axis_index("grid")

time: 453 us -> 525 us (1.16)
  waiting for transfers between devices: 271 us -> 332 us
    all_to_all x0 -> x1, waiting for transfers between devices: none -> 183 us  [shards(): pieces = lax.all_to_all(pieces, 'grid', split_axis=0, concat_axis=0)]
    all_gather x1 -> x0, waiting for transfers between devices: 123 us -> none  [shards(): group_sample = lax.all_gather(child_sample, 'grid', axis=0, tiled=True)]
where the time goes in v1:
time: 525 us
  waiting for transfers between devices  332 us (63%)
  matrix products  130 us (25%)
  local copies, waits for them, and re-layouts  41.6 us (8%)
  between operations  14.1 us (3%)
    all_to_all x1, waiting for transfers between devices, shards(): pieces = lax.all_to_all(pieces, 'grid', split_axis=0, concat_axis=0)  183 us
    all_gather x1, waiting for transfers between devices, shards(): lax.all_gather(random, ('front', 'grid'), axis=0, tiled=True)  118 us
    dot_general x1, matrix products, shards(): jnp.dot(update_front[0], child_random, preferred_element_type=jnp.float32...  58.6 us
    dot_general x1, matrix products, shards(): jnp.dot(one_hot, group_sample, preferred_element_type=jnp.float32, precis...  39 us
    gather x1, local copies, waits for them, and re-layouts, shards(): child_random = jnp.take(gathered_random, index_rows, axis=0)  37.3 us
    dot_general x1, matrix products, shards(): jnp.dot(front_matrix, gathered_random, preferred_element_type=jnp.float32...  32.3 us
    reduce_scatter x1, waiting for transfers between devices, shards(): added = lax.psum_scatter(terms, 'front', scatter_dimension=0, tiled=True)[0]  30.1 us
  transfers between devices with their start and end apart: 3, of which 3 were waited for; matrix products, arithmetic and copies ran while one was open for 0% of the time, Pallas kernels for 0%

profile of v1, /device:TPU:0, one launch (start us, length us, event | category | flops | bytes accessed | tf_op | source)
XLA Modules:
  0.0 524.8 jit_solution(2086127214786789393)
XLA Ops:
  6.5 0.0 all-gather.2.cloned.1.call-start
  6.5 0.7 all-gather.2.cloned.1.call-update
  7.9 0.8 compare_and_fusion
  8.7 0.8 compare_select_fusion
  9.5 118.0 %all-gather.2.cloned.1.call-done = f32[16384,256]{1,0:T(8,128)} async-done(((f32[512,256]{1,0:T(8,128)}), f32[16384,256]{1,0:T(8,128)}) %all-gather.2.cloned.1.call-update) | async-done | bytes 16777232 | tf_op jit(solution)/shard_map/all_gather | solution.py:8
  127.5 37.3 %gather_fusion = f32[8192,256]{1,0:T(8,128)} fusion(f32[16384,256]{1,0:T(8,128)} %all-gather.2.cloned.1.call-done, s32[8192]{0:T(1024)S(1)} %broadcast_clamp_fusion), kind=kCustom, calls=%fused_computation | custom fusion | bytes 16809984 | tf_op jit(solution)/shard_map/jit(_take)/gather | solution.py:16
  164.8 58.6 %fusion.14 = f32[1024,256]{0,1:T(8,128)S(1)} fusion(f32[1,1024,8192]{2,1,0:T(8,128)} %param.7, f32[8192,256]{1,0:T(8,128)} %gather_fusion, pred[8192]{0:T(1024)(128)(4,1)S(1)} %compare_and_fusion, pred[1024]{0:T(1024)(128)(4,1)S(1)} %add_compare_fusion), kind=kOutput, calls=%fused_computation.11 | convolution fusion | flops 25772163072 | bytes 43000832 | tf_op jit(solution)/shard_map/dot_general | solution.py:17
  223.4 0.0 copy-start
  223.4 0.3 copy.7
  223.8 3.9 stack.2
  227.7 5.0 all-to-all-start
  232.7 0.2 reduce-scatter.2.cloned.1.call-start
  232.9 0.1 iota_add_fusion
  233.0 183.4 %all-to-all-done = f32[8,1024,256]{2,1,0:T(8,128)} async-done(((f32[8,1024,256]{2,1,0:T(8,128)}), f32[8,1024,256]{2,1,0:T(8,128)}, u32[]{:S(2)}, u32[]{:S(2)}) %all-to-all-start) | async-done | bytes 8388640 | tf_op jit(solution)/shard_map/all_to_all | solution.py:31
  416.4 0.0 copy-done
  416.4 39.0 %fusion = f32[4,512,256]{2,1,0:T(8,128)} fusion(f32[8192,256,1]{1,0,2:T(8,128)} %bitcast.7, s32[8192]{0:T(1024)S(1)} %bitcast.24, s32[4,512]{1,0:T(4,128)S(1)} %iota_add_fusion), kind=kOutput, calls=%fused_computation.1 | convolution fusion | flops 51556384768 | bytes 10526720 | tf_op jit(solution)/shard_map/dot_general | solution.py:39
  455.5 0.0 reduce-scatter.2.cloned.1.call-update
  455.5 30.1 %reduce-scatter.2.cloned.1.call-done = f32[1,512,256]{2,1,0:T(8,128)} async-done(((f32[4,512,256]{2,1,0:T(8,128)}), f32[1,512,256]{2,1,0:T(8,128)}) %reduce-scatter.2.cloned.1.call-update) | async-done | bytes 524304 | tf_op jit(solution)/shard_map/reduce_scatter | solution.py:43
  485.6 32.3 %convolution_add_fusion = f32[512,256]{1,0:T(8,128)} fusion(f32[512,16384]{1,0:T(8,128)} %param.8, f32[16384,256]{1,0:T(8,128)} %all-gather.2.cloned.1.call-done, f32[1,512,256]{2,1,0:T(8,128)} %reduce-scatter.2.cloned.1.call-done), kind=kOutput, calls=%fused_computation.12 | convolution fusion | flops 25769934848 | bytes 51380224 | tf_op jit(solution)/shard_map/dot_general | solution.py:9
  (3 shorter events, 0.0 us)
Async XLA Ops:
  6.5 121.0 %all-gather.2.cloned.1.call-start = ((), (), s32[]{:S(2)}) async-start(), calls=%async_computation.2 | async-start | bytes 17301504 | tf_op jit(solution)/shard_map/all_gather | solution.py:8
  223.4 193.0 %copy-start = (s32[1,8192]{1,0:T(1,128)S(1)}, s32[1,8192]{1,0:T(1,128)}, u32[]{:S(2)}) copy-start(s32[1,8192]{1,0:T(1,128)} %param.5) | copy-start | bytes 98308
  227.7 188.7 %all-to-all-start = ((f32[8,1024,256]{2,1,0:T(8,128)}), f32[8,1024,256]{2,1,0:T(8,128)}, u32[]{:S(2)}, u32[]{:S(2)}) async-start(f32[8,1024,256]{2,1,0:T(8,128)} %stack.2), calls=%async_computation | async-start | bytes 16777216 | tf_op jit(solution)/shard_map/all_to_all | solution.py:31
  232.7 252.9 %reduce-scatter.2.cloned.1.call-start = ((), (), s32[]{:S(2)}) async-start(), calls=%async_computation.3 | async-start | bytes 2621440 | tf_op jit(solution)/shard_map/reduce_scatter | solution.py:43
Sparse Core Ops, SparseCore 0:
  10.4 117.0 all-gather.1
  455.6 29.9 reduce-scatter.1
